TPU v7x, 32 devices: a whole 2x2x4 slice. The times are simulated.
32 devices in a mesh: space: 8 (over z, y), level: 4 (over x, core).
Axes of the slice: x: 2, y: 2, z: 4, core: 2. Of those that a mesh axis runs over, the one named last changes fastest.
Arguments:
- grid_latent: bfloat16 [4096, 512], P('space'), may hold values from -6 to 6
- mesh_latent: bfloat16 [4, 64, 512], P('level', 'space'), may hold values from -6 to 6
- grid_output_cotangent: bfloat16 [4096, 512], P('space'), may hold values from -6 to 6
- w_send: bfloat16 [512, 512], replicated, may hold values from -0.25 to 0.25
- w_recv: bfloat16 [512, 512], replicated, may hold values from -0.25 to 0.25
- output_weight: bfloat16 [512, 512], replicated, may hold values from -0.25 to 0.25
- hidden_layer_bias: float32 [512], replicated, may hold values from -4 to 4
- output_norm_gain: float32 [512], replicated, may hold values from 0.1 to 1.9
- edge_sender: int32 [4, 16384], P('level', 'space'), may hold values from 0 to 23
- edge_receiver: int32 [4, 16384], P('level', 'space'), may hold values from 0 to 511
- edge_live: int32 [4, 16384], P('level', 'space'), may hold values 0 or 1
Outputs:
- d_grid: float32 [4096, 512], P(('space', 'level'))
- d_mesh: float32 [4, 64, 512], P('level', 'space')
- d_w_send: bfloat16 [512, 512], replicated
- d_w_recv: bfloat16 [512, 512], replicated
- d_w_out: bfloat16 [512, 512], replicated
- d_bias: float32 [512], replicated
- d_gain: float32 [512], replicated
All inputs are finite; a program needn't handle non-finite values. No bound on the sum of `edge_live` on one device may be relied on, other than what follows from the above.
Results may differ from a plain program's by a relative error of at most 0.012.
Values may be sent and summed in bfloat16 or wider, within the bound.
No kernel may reach another device: no remote copies, remote signals or barrier semaphores. Data moves between devices by JAX's collectives and lax.ppermute only.
A program may use at most 64 MiB of HBM per device.

v0:
```python
import jax
import jax.numpy as jnp
from jax import lax
from jax.sharding import PartitionSpec as P


def with_halo(cells, sides, width):
    for axis, dim in sides:
        count = lax.axis_size(axis)
        ends = count - 1
        head = lax.slice_in_dim(cells, 0, width, axis=dim)
        tail = lax.slice_in_dim(cells, cells.shape[dim] - width, cells.shape[dim], axis=dim)
        cells = jnp.concatenate(
            [
                lax.ppermute(tail, axis, [(i, (i + 1) % count) for i in range(ends)]),
                cells,
                lax.ppermute(head, axis, [((i + 1) % count, i) for i in range(ends)]),
            ],
            axis=dim,
        )
    return cells


def from_behind(block, axis, distance):
    devices = range(lax.axis_size(axis))
    route = [(i - distance, i) for i in devices if i - distance in devices]
    return lax.ppermute(block, axis, route)


def edge_reverse_step(
    sending_rows,
    receiver_rows,
    cotangent_lines,
    slot_active_flags,
    output_weight,
    hidden_layer_bias,
    output_norm_gain,
):
    preact = sending_rows + receiver_rows + hidden_layer_bias
    hidden = jax.nn.silu(preact).astype(jnp.bfloat16)
    outer = jnp.dot(hidden, output_weight, preferred_element_type=jnp.float32)
    center = outer - jnp.mean(outer, axis=-1, keepdims=True)
    inv_scale = lax.rsqrt(jnp.mean(center * center, axis=-1, keepdims=True) + 1e-05)
    normed = center * inv_scale
    incoming_gradient = cotangent_lines.astype(jnp.float32) * slot_active_flags[:, None].astype(
        jnp.float32
    )
    scaled = incoming_gradient * output_norm_gain
    d_outer = inv_scale * (
        scaled
        - jnp.mean(scaled, axis=-1, keepdims=True)
        - normed * jnp.mean(scaled * normed, axis=-1, keepdims=True)
    )
    d_outer_b = d_outer.astype(jnp.bfloat16)
    w_out_grad = jnp.dot(hidden.T, d_outer_b, preferred_element_type=jnp.float32)
    d_hidden = jnp.dot(d_outer_b, output_weight.T, preferred_element_type=jnp.float32)
    sigmoid = jax.nn.sigmoid(preact)
    preactivation_gradient = d_hidden * sigmoid * (1.0 + preact * (1.0 - sigmoid))
    return (
        preactivation_gradient,
        w_out_grad,
        jnp.sum(preactivation_gradient, axis=0),
        jnp.sum(incoming_gradient * normed, axis=0),
    )


def body(
    grid_latent,
    mesh_latent,
    grid_output_cotangent,
    w_send,
    w_recv,
    output_weight,
    hidden_layer_bias,
    output_norm_gain,
    edge_sender,
    edge_receiver,
    edge_live,
):
    shards = lax.axis_size("space")
    width = grid_latent.shape[1]
    grid_rows = grid_latent.shape[0]
    mesh_rows = mesh_latent.shape[1]
    slots = edge_sender.shape[1]
    sender_local = edge_sender[0]
    receiver_index = edge_receiver[0]
    band = lax.axis_index("space")
    window = sender_local // mesh_rows
    target = band + window - 1
    inside = (target >= 0) & (target < shards)
    window = jnp.where(inside, window, 1)
    table_row = window * mesh_rows + sender_local % mesh_rows
    proj_send = jnp.dot(mesh_latent[0], w_send, preferred_element_type=jnp.float32).astype(
        jnp.bfloat16
    )
    projected_receiver = jnp.dot(grid_latent, w_recv, preferred_element_type=jnp.float32)
    table = with_halo(proj_send, (("space", 0),), mesh_rows)
    sending_rows = table[table_row]
    block = 512
    blocks = slots // block

    def run_block(operands):
        rows_send, rows_recv, rows_cot, rows_live = operands
        return edge_reverse_step(
            rows_send.astype(jnp.float32),
            rows_recv,
            rows_cot,
            rows_live,
            output_weight,
            hidden_layer_bias,
            output_norm_gain,
        )

    operands = (
        sending_rows.reshape(blocks, block, width),
        projected_receiver[receiver_index].reshape(blocks, block, width),
        grid_output_cotangent[receiver_index].reshape(blocks, block, width),
        edge_live[0].reshape(blocks, block),
    )
    d_pre_blocks, wout_blocks, bias_blocks, gain_blocks = lax.map(run_block, operands)
    preactivation_gradient = d_pre_blocks.reshape(slots, width)
    output_weight_piece = jnp.sum(wout_blocks, axis=0)
    bias_piece = jnp.sum(bias_blocks, axis=0)
    gain_piece = jnp.sum(gain_blocks, axis=0)
    table_grads = jax.ops.segment_sum(preactivation_gradient, table_row, num_segments=3 * mesh_rows)
    below = table_grads[:mesh_rows]
    above = table_grads[2 * mesh_rows :]
    from_below = from_behind(above, "space", 1)
    from_above = from_behind(below, "space", -1)
    mesh_acc = table_grads[mesh_rows : 2 * mesh_rows] + from_below + from_above
    grid_local = jax.ops.segment_sum(preactivation_gradient, receiver_index, num_segments=grid_rows)
    share = grid_rows // lax.axis_size("level")
    offset = lax.axis_index("level") * share
    grid_acc = lax.psum_scatter(
        grid_local.astype(jnp.bfloat16), "level", scatter_dimension=0, tiled=True
    )
    grid_part = lax.dynamic_slice_in_dim(grid_latent, offset, share, 0)
    mesh_sum = mesh_acc.astype(jnp.bfloat16)
    d_mesh = jnp.dot(mesh_sum, w_send.T, preferred_element_type=jnp.float32)[None]
    d_grid = jnp.dot(grid_acc, w_recv.T, preferred_element_type=jnp.float32)
    wsend_part = jnp.dot(mesh_latent[0].T, mesh_sum, preferred_element_type=jnp.float32)
    wrecv_part = jnp.dot(grid_part.T, grid_acc, preferred_element_type=jnp.float32)
    totals = lax.psum(
        (wsend_part, wrecv_part, output_weight_piece, bias_piece, gain_piece), ("space", "level")
    )
    d_w_send = totals[0].astype(jnp.bfloat16)
    d_w_recv = totals[1].astype(jnp.bfloat16)
    d_w_out = totals[2].astype(jnp.bfloat16)
    d_bias = totals[3]
    d_gain = totals[4]
    return (d_grid, d_mesh, d_w_send, d_w_recv, d_w_out, d_bias, d_gain)


def solution(mesh):
    return jax.shard_map(
        body,
        mesh=mesh,
        in_specs=(
            P("space", None),
            P("level", "space", None),
            P("space", None),
            P(),
            P(),
            P(),
            P(),
            P(),
            P("level", "space"),
            P("level", "space"),
            P("level", "space"),
        ),
        out_specs=(P(("space", "level"), None), P("level", "space", None), P(), P(), P(), P(), P()),
        check_vma=False,
    )
```

profile of v0, /device:TPU:0, one launch (start us, length us, event | category | flops | bytes accessed | tf_op | source)
XLA Modules:
  0.0 218.6 jit_solution(9644242598406611209)
XLA Ops:
  7.2 1.3 convolution_convert_fusion
  8.5 1.3 collective-permute-start.1
  9.8 5.5 %collective-permute-start = (bf16[8,512]{1,0:T(8,128)(2,1)S(1)}, bf16[8,512]{1,0:T(8,128)(2,1)S(1)}, u32[]{:S(2)}, u32[]{:S(2)}) collective-permute-start(bf16[8,512]{1,0:T(8,128)(2,1)S(1)} %convolution_convert_fusion), channel_id=1, source_target_pairs={{0,4},{4,8},{8,12},{12,16},{16,20},{20,24},{24,28},{1,5},{5,9},{9,... | collective-permute-start | bytes 24584 | tf_op jit(solution)/shard_map/ppermute | solution.py:15
  16.9 1.6 fusion.27
  19.1 1.4 reduce.3
  20.5 9.2 %gather_fusion.2 = bf16[2048,512]{1,0:T(8,128)(2,1)} fusion(bf16[512,512]{1,0:T(8,128)(2,1)S(1)} %copy-done, s32[2048]{0:T(1024)S(1)} %broadcast_clamp_fusion), kind=kCustom, calls=%fused_computation.2 | custom fusion | bytes 4202496 | tf_op jit(solution)/shard_map/gather | solution.py:117
  29.6 8.9 %gather_fusion.1 = f32[2048,512]{1,0:T(8,128)} fusion(f32[512,512]{1,0:T(8,128)S(1)} %fusion.27, s32[2048]{0:T(1024)S(1)} %broadcast_clamp_fusion), kind=kCustom, calls=%fused_computation.1 | custom fusion | bytes 8396800 | tf_op jit(solution)/shard_map/gather | solution.py:116
  38.6 9.2 %gather_fusion = bf16[2048,512]{1,0:T(8,128)(2,1)} fusion(bf16[24,512]{1,0:T(8,128)(2,1)S(1)} %pad_maximum_fusion, s32[2048]{0:T(1024)S(1)} %broadcast_clamp_fusion.1), kind=kCustom, calls=%fused_computation | custom fusion | bytes 4202496 | tf_op jit(solution)/shard_map/gather | solution.py:98
  47.8 37.2 %while.16 = (s32[]{:T(128)}, f32[4,512,512]{2,1,0:T(8,128)}, f32[4,512,512]{2,1,0:T(8,128)}, f32[4,512]{1,0:T(4,128)S(1)}, f32[4,512]{1,0:T(4,128)S(1)}, /*index...) while((s32[]{:T(128)}, f32[4,512,512]{2,1,0:T(8,128)}, ...), condition=%wide.region_7.8_spmd, body=%wide.region_0.7_spmd.sunk | while | flops 816840704 | bytes 18942132 | solution.py:120
  47.8 1.7 multiply_convert_fusion.2
  49.5 1.1 constant_dynamic-slice_fusion.2
  52.3 1.6 fusion.63
  53.9 3.0 %bitcast_dynamic-update-slice_fusion.2 = (f32[4,512,512]{2,1,0:T(8,128)}, f32[512,512]{1,0:T(8,128)S(1)}) fusion(f32[4,512,512]{2,1,0:T(8,128)} %get-tuple-element.263, s32[]{:T(128)S(6)} %copy.34, f32[512]{0:T(512)S(1)} %get-tuple-element.284, f32[4,512,512]{2,1,0:T(8,128)} %get-tuple-element.283, bf16[4,512,512]{2,1,0:T(8,128)(2,1)} %get-tuple-element.282, ...), kind=kOutput, calls=%fused_computation.20.clone.1 | convolution fusion | flops 271319040 | bytes 4720644 | tf_op jit(solution)/shard_map/while/body/eval_jaxpr/dot_general | solution.py:56
  57.1 1.7 multiply_convert_fusion.2
  58.8 1.1 constant_dynamic-slice_fusion.2
  61.7 1.5 fusion.63
  63.2 3.1 %bitcast_dynamic-update-slice_fusion.2 = (f32[4,512,512]{2,1,0:T(8,128)}, f32[512,512]{1,0:T(8,128)S(1)}) fusion(f32[4,512,512]{2,1,0:T(8,128)} %get-tuple-element.263, s32[]{:T(128)S(6)} %copy.34, f32[512]{0:T(512)S(1)} %get-tuple-element.284, f32[4,512,512]{2,1,0:T(8,128)} %get-tuple-element.283, bf16[4,512,512]{2,1,0:T(8,128)(2,1)} %get-tuple-element.282, ...), kind=kOutput, calls=%fused_computation.20.clone.1 | convolution fusion | flops 271319040 | bytes 4720644 | tf_op jit(solution)/shard_map/while/body/eval_jaxpr/dot_general | solution.py:56
  66.4 1.7 multiply_convert_fusion.2
  68.1 1.1 constant_dynamic-slice_fusion.2
  71.0 1.5 fusion.63
  72.5 3.1 %bitcast_dynamic-update-slice_fusion.2 = (f32[4,512,512]{2,1,0:T(8,128)}, f32[512,512]{1,0:T(8,128)S(1)}) fusion(f32[4,512,512]{2,1,0:T(8,128)} %get-tuple-element.263, s32[]{:T(128)S(6)} %copy.34, f32[512]{0:T(512)S(1)} %get-tuple-element.284, f32[4,512,512]{2,1,0:T(8,128)} %get-tuple-element.283, bf16[4,512,512]{2,1,0:T(8,128)(2,1)} %get-tuple-element.282, ...), kind=kOutput, calls=%fused_computation.20.clone.1 | convolution fusion | flops 271319040 | bytes 4720644 | tf_op jit(solution)/shard_map/while/body/eval_jaxpr/dot_general | solution.py:56
  75.7 1.7 multiply_convert_fusion.2
  80.3 1.5 fusion.63
  81.7 3.0 %bitcast_dynamic-update-slice_fusion.2 = (f32[4,512,512]{2,1,0:T(8,128)}, f32[512,512]{1,0:T(8,128)S(1)}) fusion(f32[4,512,512]{2,1,0:T(8,128)} %get-tuple-element.263, s32[]{:T(128)S(6)} %copy.34, f32[512]{0:T(512)S(1)} %get-tuple-element.284, f32[4,512,512]{2,1,0:T(8,128)} %get-tuple-element.283, bf16[4,512,512]{2,1,0:T(8,128)(2,1)} %get-tuple-element.282, ...), kind=kOutput, calls=%fused_computation.20.clone.1 | convolution fusion | flops 271319040 | bytes 4720644 | tf_op jit(solution)/shard_map/while/body/eval_jaxpr/dot_general | solution.py:56
  84.9 13.5 %scatter_custom_fusion = f32[512,512]{1,0:T(8,128)S(1)} fusion(s32[2048]{0:T(1024)} %bitcast.107, f32[2048,512]{1,0:T(8,128)} %bitcast.108, f32[]{:T(128)} %constant.75.clone.1), kind=kCustom, calls=%fused_computation.35 | custom fusion | flops 1048576 | bytes 1049088 | tf_op jit(solution)/shard_map/scatter-add | solution.py:131
  99.3 13.2 %scatter_custom_fusion.1 = f32[24,512]{1,0:T(8,128)S(1)} fusion(s32[2048]{0:T(1024)S(1)} %bitcast.106, f32[2048,512]{1,0:T(8,128)} %bitcast.109, f32[]{:T(128)} %constant.75.clone.1), kind=kCustom, calls=%fused_computation.45 | custom fusion | flops 1048576 | bytes 49664 | tf_op jit(solution)/shard_map/scatter-add | solution.py:125
  112.6 4.8 %collective-permute-start.2 = (f32[8,512]{1,0:T(8,128)S(1)}, f32[8,512]{1,0:T(8,128)S(1)}, u32[]{:S(2)}, u32[]{:S(2)}) collective-permute-start(f32[8,512]{1,0:T(8,128)S(1)} %get-tuple-element.154), channel_id=1, source_target_pairs={{0,4},{4,8},{8,12},{12,16},{16,20},{20,24},{24,28},{1,5},{5,9},{9,... | collective-permute-start | bytes 49160 | tf_op jit(solution)/shard_map/ppermute | solution.py:27
  117.4 1.5 collective-permute-start.3
  118.9 3.8 %reduce_sum.81 = f32[512,512]{1,0:T(8,128)} reduce(f32[4,512,512]{2,1,0:T(8,128)} %get-tuple-element.73, f32[]{:T(128)} %constant.75.clone.1), dimensions={0}, to_apply=%region_13.14 | reduce | flops 786432 | bytes 5242884 | tf_op jit(solution)/shard_map/reduce_sum | solution.py:122
  124.3 1.3 fusion.14
  125.6 83.1 %all-reduce.2 = (bf16[512,512]{0,1:T(8,128)(2,1)}, bf16[512,512]{1,0:T(8,128)(2,1)}, bf16[512,512]{1,0:T(8,128)(2,1)}, f32[512]{0:T(512)}, f32[512]{0:T(512)}) all-reduce(f32[512,512]{0,1:T(8,128)S(1)} %convolution_bitcast_fusion.1, f32[512,512]{1,0:T(8,128)S(1)} %fusion.14, ...), channel_id=1, replica_groups=mesh['space'=8,'level'=4] {'space','level'}, use_global_device_ids=true, to_apply=%region_11.12 | all-reduce | flops 787456 | bytes 4726784 | tf_op jit(solution)/shard_map/psum | solution.py:143
  208.7 2.0 copy.21
  (91 shorter events, 14.4 us)
Async XLA Ops:
  7.2 13.3 %copy-start = (bf16[512,512]{1,0:T(8,128)(2,1)S(1)}, bf16[512,512]{1,0:T(8,128)(2,1)}, u32[]{:S(2)}) copy-start(bf16[512,512]{1,0:T(8,128)(2,1)} %param.15) | copy-start | bytes 1572868
  7.2 117.1 %reduce-scatter.2.cloned.1.call-start = ((), (), s32[]{:S(2)}) async-start(), calls=%async_computation.1 | async-start | bytes 655360 | tf_op jit(solution)/shard_map/reduce_scatter | solution.py:134
  8.5 30.0 %collective-permute-start.1 = (bf16[8,512]{1,0:T(8,128)(2,1)S(1)}, bf16[8,512]{1,0:T(8,128)(2,1)S(1)}, u32[]{:S(2)}, u32[]{:S(2)}) collective-permute-start(bf16[8,512]{1,0:T(8,128)(2,1)S(1)} %convolution_convert_fusion), channel_id=1, source_target_pairs={{4,0},{8,4},{12,8},{16,12},{20,16},{24,20},{28,24},{5,1},{9,5},{13... | collective-permute-start | bytes 24584 | tf_op jit(solution)/shard_map/ppermute | solution.py:17
  9.8 28.7 %collective-permute-start = (bf16[8,512]{1,0:T(8,128)(2,1)S(1)}, bf16[8,512]{1,0:T(8,128)(2,1)S(1)}, u32[]{:S(2)}, u32[]{:S(2)}) collective-permute-start(bf16[8,512]{1,0:T(8,128)(2,1)S(1)} %convolution_convert_fusion), channel_id=1, source_target_pairs={{0,4},{4,8},{8,12},{12,16},{16,20},{20,24},{24,28},{1,5},{5,9},{9,... | collective-permute-start | bytes 24584 | tf_op jit(solution)/shard_map/ppermute | solution.py:15
  38.5 9.2 %copy-start.1 = (bf16[512,512]{1,0:T(8,128)(2,1)S(1)}, bf16[512,512]{1,0:T(8,128)(2,1)}, u32[]{:S(2)}) copy-start(bf16[512,512]{1,0:T(8,128)(2,1)} %param.18) | copy-start | bytes 1572868
  38.5 9.2 %copy-start.5 = (f32[512]{0:T(512)S(1)}, f32[512]{0:T(512)}, u32[]{:S(2)}) copy-start(f32[512]{0:T(512)} %param.20) | copy-start | bytes 6148
  38.5 9.2 %copy-start.6 = (f32[512]{0:T(512)S(1)}, f32[512]{0:T(512)}, u32[]{:S(2)}) copy-start(f32[512]{0:T(512)} %param.19) | copy-start | bytes 6148
  84.9 38.1 %copy-start.7 = (bf16[1,8,512]{2,1,0:T(8,128)(2,1)S(1)}, bf16[1,8,512]{2,1,0:T(8,128)(2,1)}, u32[]{:S(2)}) copy-start(bf16[1,8,512]{2,1,0:T(8,128)(2,1)} %param.14) | copy-start | bytes 24580
  98.4 25.0 %copy-start.2 = (bf16[512,512]{1,0:T(8,128)(2,1)S(1)}, bf16[512,512]{1,0:T(8,128)(2,1)}, u32[]{:S(2)}) copy-start(bf16[512,512]{1,0:T(8,128)(2,1)} %param.16) | copy-start | bytes 1572868
  112.6 10.1 %collective-permute-start.2 = (f32[8,512]{1,0:T(8,128)S(1)}, f32[8,512]{1,0:T(8,128)S(1)}, u32[]{:S(2)}, u32[]{:S(2)}) collective-permute-start(f32[8,512]{1,0:T(8,128)S(1)} %get-tuple-element.154), channel_id=1, source_target_pairs={{0,4},{4,8},{8,12},{12,16},{16,20},{20,24},{24,28},{1,5},{5,9},{9,... | collective-permute-start | bytes 49160 | tf_op jit(solution)/shard_map/ppermute | solution.py:27
  117.4 5.6 %collective-permute-start.3 = (f32[8,512]{1,0:T(8,128)S(1)}, f32[8,512]{1,0:T(8,128)S(1)}, u32[]{:S(2)}, u32[]{:S(2)}) collective-permute-start(f32[8,512]{1,0:T(8,128)S(1)} %get-tuple-element.155), channel_id=1, source_target_pairs={{4,0},{8,4},{12,8},{16,12},{20,16},{24,20},{28,24},{5,1},{9,5},{13... | collective-permute-start | bytes 49160 | tf_op jit(solution)/shard_map/ppermute | solution.py:27
  122.7 88.0 %copy-start.3 = (bf16[512,512]{1,0:T(8,128)(2,1)S(1)}, bf16[512,512]{1,0:T(8,128)(2,1)}, u32[]{:S(2)}) copy-start(bf16[512,512]{1,0:T(8,128)(2,1)} %param.17) | copy-start | bytes 1572868
  124.3 86.5 %copy-start.4 = (bf16[128,512]{1,0:T(8,128)(2,1)S(1)}, bf16[128,512]{1,0:T(8,128)(2,1)}, u32[]{:S(2)}) copy-start(bf16[128,512]{1,0:T(8,128)(2,1)} %reduce-scatter.2.cloned.1.call-done) | copy-start | bytes 393220
Sparse Core Ops, SparseCore 0:
  99.4 23.2 reduce-scatter.1
where the time goes:
time: 220 us; the launch traced here: 219 us
  blocking collectives  83.1 us (38%)
  other arithmetic  45.5 us (21%)
  local copies, waits for them, and re-layouts  35.4 us (16%)
  matrix products  26.6 us (12%)
  between operations  14.3 us (6%)
  starting transfers between devices  13.2 us (6%)
    psum x1, blocking collectives, body(): lax.psum((wsend_part, wrecv_part, output_weight_piece, bias_piece, gain_p...  83.1 us
    scatter-add x1, other arithmetic, body(): jax.ops.segment_sum(preactivation_gradient, receiver_index, num_segments=...  13.5 us
    scatter-add x1, other arithmetic, body(): jax.ops.segment_sum(preactivation_gradient, table_row, num_segments=3 * m...  13.2 us
    dot_general x4, matrix products, edge_reverse_step(): jnp.dot(d_outer_b, output_weight.T, preferred_element_type=jnp.float32)  12.2 us
    gather x1, local copies, waits for them, and re-layouts, body(): sending_rows = table[table_row]  9.18 us
    gather x1, local copies, waits for them, and re-layouts, body(): grid_output_cotangent[receiver_index].reshape(blocks, block, width)  9.15 us
    gather x1, local copies, waits for them, and re-layouts, body(): projected_receiver[receiver_index].reshape(blocks, block, width)  8.9 us
    convert_element_type x4, other arithmetic, edge_reverse_step(): hidden = jax.nn.silu(preact).astype(jnp.bfloat16)  6.68 us
  transfers between devices with their start and end apart: 5, of which 1 were waited for; matrix products, arithmetic and copies ran while one was open for 19% of the time, Pallas kernels for 0%

commit v1 on v0

--- a/solution.py
+++ b/solution.py
@@ -140,9 +140,9 @@
     d_grid = jnp.dot(grid_acc, w_recv.T, preferred_element_type=jnp.float32)
     wsend_part = jnp.dot(mesh_latent[0].T, mesh_sum, preferred_element_type=jnp.float32)
     wrecv_part = jnp.dot(grid_part.T, grid_acc, preferred_element_type=jnp.float32)
-    totals = lax.psum(
-        (wsend_part, wrecv_part, output_weight_piece, bias_piece, gain_piece), ("space", "level")
-    )
+    totals = (wsend_part, wrecv_part, output_weight_piece, bias_piece, gain_piece)
+    for name in ("level", "space"):
+        totals = lax.psum(totals, name)
     d_w_send = totals[0].astype(jnp.bfloat16)
     d_w_recv = totals[1].astype(jnp.bfloat16)
     d_w_out = totals[2].astype(jnp.bfloat16)

time: 220 us -> 336 us (1.53)
  waiting for transfers between devices: 0.36 us -> 62.6 us
  blocking collectives: 83.1 us -> 136 us
    psum x0 -> x1, waiting for transfers between devices: none -> 62.2 us  [body(): totals = lax.psum(totals, name)]
    psum x1 -> x2, blocking collectives: 83.1 us -> 136 us  [body(): totals = lax.psum(totals, name)]
  transfers between devices with their start and end apart: 5 -> 6, of which waited for: 1 -> 2; matrix products, arithmetic and copies ran while one was open for 19% -> 13% of each run, Pallas kernels for 0% -> 0%
where the time goes in v1:
time: 336 us; the launch traced here: 335 us
  blocking collectives  136 us (40%)
  waiting for transfers between devices  62.6 us (19%)
  other arithmetic  45.5 us (14%)
  local copies, waits for them, and re-layouts  34.4 us (10%)
  matrix products  28.6 us (9%)
  between operations  14.3 us (4%)
  starting transfers between devices  13.2 us (4%)
    psum x2, blocking collectives, body(): totals = lax.psum(totals, name)  136 us
    psum x1, waiting for transfers between devices, body(): totals = lax.psum(totals, name)  62.2 us
    scatter-add x1, other arithmetic, body(): jax.ops.segment_sum(preactivation_gradient, receiver_index, num_segments=...  13.5 us
    scatter-add x1, other arithmetic, body(): jax.ops.segment_sum(preactivation_gradient, table_row, num_segments=3 * m...  13.2 us
    dot_general x4, matrix products, edge_reverse_step(): jnp.dot(d_outer_b, output_weight.T, preferred_element_type=jnp.float32)  12.2 us
    gather x1, local copies, waits for them, and re-layouts, body(): sending_rows = table[table_row]  9.18 us
    gather x1, local copies, waits for them, and re-layouts, body(): grid_output_cotangent[receiver_index].reshape(blocks, block, width)  9.15 us
    gather x1, local copies, waits for them, and re-layouts, body(): projected_receiver[receiver_index].reshape(blocks, block, width)  8.9 us
  transfers between devices with their start and end apart: 6, of which 2 were waited for; matrix products, arithmetic and copies ran while one was open for 13% of the time, Pallas kernels for 0%

profile of v1, /device:TPU:0, one launch (start us, length us, event | category | flops | bytes accessed | tf_op | source)
XLA Modules:
  0.0 334.9 jit_solution(3485178069087858192)
XLA Ops:
  7.2 1.3 convolution_convert_fusion
  8.5 1.3 collective-permute-start.1
  9.8 5.5 %collective-permute-start = (bf16[8,512]{1,0:T(8,128)(2,1)S(1)}, bf16[8,512]{1,0:T(8,128)(2,1)S(1)}, u32[]{:S(2)}, u32[]{:S(2)}) collective-permute-start(bf16[8,512]{1,0:T(8,128)(2,1)S(1)} %convolution_convert_fusion), channel_id=1, source_target_pairs={{0,4},{4,8},{8,12},{12,16},{16,20},{20,24},{24,28},{1,5},{5,9},{9,... | collective-permute-start | bytes 24584 | tf_op jit(solution)/shard_map/ppermute | solution.py:15
  16.9 1.6 fusion.27
  19.1 1.4 reduce.3
  20.5 9.2 %gather_fusion.2 = bf16[2048,512]{1,0:T(8,128)(2,1)} fusion(bf16[512,512]{1,0:T(8,128)(2,1)S(1)} %copy-done, s32[2048]{0:T(1024)S(1)} %broadcast_clamp_fusion), kind=kCustom, calls=%fused_computation.2 | custom fusion | bytes 4202496 | tf_op jit(solution)/shard_map/gather | solution.py:117
  29.6 8.9 %gather_fusion.1 = f32[2048,512]{1,0:T(8,128)} fusion(f32[512,512]{1,0:T(8,128)S(1)} %fusion.27, s32[2048]{0:T(1024)S(1)} %broadcast_clamp_fusion), kind=kCustom, calls=%fused_computation.1 | custom fusion | bytes 8396800 | tf_op jit(solution)/shard_map/gather | solution.py:116
  38.6 9.2 %gather_fusion = bf16[2048,512]{1,0:T(8,128)(2,1)} fusion(bf16[24,512]{1,0:T(8,128)(2,1)S(1)} %pad_maximum_fusion, s32[2048]{0:T(1024)S(1)} %broadcast_clamp_fusion.1), kind=kCustom, calls=%fused_computation | custom fusion | bytes 4202496 | tf_op jit(solution)/shard_map/gather | solution.py:98
  47.8 37.2 %while.16 = (s32[]{:T(128)}, f32[4,512,512]{2,1,0:T(8,128)}, f32[4,512,512]{2,1,0:T(8,128)}, f32[4,512]{1,0:T(4,128)S(1)}, f32[4,512]{1,0:T(4,128)S(1)}, /*index...) while((s32[]{:T(128)}, f32[4,512,512]{2,1,0:T(8,128)}, ...), condition=%wide.region_7.8_spmd, body=%wide.region_0.7_spmd.sunk | while | flops 816840704 | bytes 18942132 | solution.py:120
  47.8 1.7 multiply_convert_fusion.2
  49.5 1.1 constant_dynamic-slice_fusion.2
  52.3 1.6 fusion.63
  53.9 3.0 bitcast_dynamic-update-slice_fusion.2
  57.1 1.7 multiply_convert_fusion.2
  61.7 1.5 fusion.63
  63.2 3.1 bitcast_dynamic-update-slice_fusion.2
  66.4 1.7 multiply_convert_fusion.2
  71.0 1.5 fusion.63
  72.5 3.1 bitcast_dynamic-update-slice_fusion.2
  75.7 1.7 multiply_convert_fusion.2
  80.3 1.5 fusion.63
  81.7 3.0 bitcast_dynamic-update-slice_fusion.2
  84.9 13.5 %scatter_custom_fusion = f32[512,512]{1,0:T(8,128)S(1)} fusion(s32[2048]{0:T(1024)} %bitcast.107, f32[2048,512]{1,0:T(8,128)} %bitcast.108, f32[]{:T(128)} %constant.75.clone.1), kind=kCustom, calls=%fused_computation.35 | custom fusion | flops 1048576 | bytes 1049088 | tf_op jit(solution)/shard_map/scatter-add | solution.py:131
  99.4 13.2 %scatter_custom_fusion.1 = f32[24,512]{1,0:T(8,128)S(1)} fusion(s32[2048]{0:T(1024)S(1)} %bitcast.106, f32[2048,512]{1,0:T(8,128)} %bitcast.109, f32[]{:T(128)} %constant.75.clone.1), kind=kCustom, calls=%fused_computation.45 | custom fusion | flops 1048576 | bytes 49664 | tf_op jit(solution)/shard_map/scatter-add | solution.py:125
  112.6 4.8 %collective-permute-start.2 = (f32[8,512]{1,0:T(8,128)S(1)}, f32[8,512]{1,0:T(8,128)S(1)}, u32[]{:S(2)}, u32[]{:S(2)}) collective-permute-start(f32[8,512]{1,0:T(8,128)S(1)} %get-tuple-element.159), channel_id=1, source_target_pairs={{0,4},{4,8},{8,12},{12,16},{16,20},{20,24},{24,28},{1,5},{5,9},{9,... | collective-permute-start | bytes 49160 | tf_op jit(solution)/shard_map/ppermute | solution.py:27
  117.4 1.5 collective-permute-start.3
  118.9 3.8 %reduce_sum.81 = f32[512,512]{1,0:T(8,128)} reduce(f32[4,512,512]{2,1,0:T(8,128)} %get-tuple-element.73, f32[]{:T(128)} %constant.75.clone.1), dimensions={0}, to_apply=%region_15.16 | reduce | flops 786432 | bytes 5242884 | tf_op jit(solution)/shard_map/reduce_sum | solution.py:122
  123.1 1.3 convolution_bitcast_fusion.1
  124.4 2.3 fusion.14
  126.8 5.7 %all-reduce.1 = (f32[512]{0:T(512)S(1)}, f32[512]{0:T(512)S(1)}) all-reduce(f32[512]{0:T(512)S(1)} %reduce_sum.82, f32[512]{0:T(512)S(1)} %reduce_sum.83), channel_id=1, replica_groups=mesh['space'=8,'level'=4] {'level'}, use_global_device_ids=true, to_apply=%region_19.20 | all-reduce | flops 1024 | bytes 8192 | tf_op jit(solution)/shard_map/psum | solution.py:145
  134.4 62.2 %all-reduce.6.cloned.1.call-done = (f32[512,512]{0,1:T(8,128)}, f32[512,512]{1,0:T(8,128)}, f32[512,512]{1,0:T(8,128)}) async-done(((f32[512,512]{0,1:T(8,128)}, f32[512,512]{1,0:T(8,128)}, f32[512,512]{1,0:T(8,128)}), (f32[512,512]{0,1:T(8,128)}, f32[512,512]{1,0:T(8,128)}, f32[512,512]{1,0:T(8,128)})) %all-reduce.6.cloned.1.call-update) | async-done | bytes 3145744 | tf_op jit(solution)/shard_map/psum | solution.py:145
  196.6 130.5 %all-reduce.7 = (bf16[512,512]{0,1:T(8,128)(2,1)S(1)}, bf16[512,512]{1,0:T(8,128)(2,1)}, bf16[512,512]{1,0:T(8,128)(2,1)}, f32[512]{0:T(512)}, f32[512]{0:T(512)}) all-reduce(f32[512,512]{0,1:T(8,128)} %get-tuple-element.148, f32[512,512]{1,0:T(8,128)} %get-tuple-element.149, ...), channel_id=1, replica_groups=mesh['space'=8,'level'=4] {'space'}, use_global_device_ids=true, to_apply=%region_12.13 | all-reduce | flops 787456 | bytes 4726784 | tf_op jit(solution)/shard_map/psum | solution.py:145
  (95 shorter events, 17.3 us)
Async XLA Ops:
  7.2 13.3 %copy-start = (bf16[512,512]{1,0:T(8,128)(2,1)S(1)}, bf16[512,512]{1,0:T(8,128)(2,1)}, u32[]{:S(2)}) copy-start(bf16[512,512]{1,0:T(8,128)(2,1)} %param.15) | copy-start | bytes 1572868
  7.2 117.2 %reduce-scatter.2.cloned.1.call-start = ((), (), s32[]{:S(2)}) async-start(), calls=%async_computation.1 | async-start | bytes 655360 | tf_op jit(solution)/shard_map/reduce_scatter | solution.py:134
  8.5 30.0 %collective-permute-start.1 = (bf16[8,512]{1,0:T(8,128)(2,1)S(1)}, bf16[8,512]{1,0:T(8,128)(2,1)S(1)}, u32[]{:S(2)}, u32[]{:S(2)}) collective-permute-start(bf16[8,512]{1,0:T(8,128)(2,1)S(1)} %convolution_convert_fusion), channel_id=1, source_target_pairs={{4,0},{8,4},{12,8},{16,12},{20,16},{24,20},{28,24},{5,1},{9,5},{13... | collective-permute-start | bytes 24584 | tf_op jit(solution)/shard_map/ppermute | solution.py:17
  9.8 28.7 %collective-permute-start = (bf16[8,512]{1,0:T(8,128)(2,1)S(1)}, bf16[8,512]{1,0:T(8,128)(2,1)S(1)}, u32[]{:S(2)}, u32[]{:S(2)}) collective-permute-start(bf16[8,512]{1,0:T(8,128)(2,1)S(1)} %convolution_convert_fusion), channel_id=1, source_target_pairs={{0,4},{4,8},{8,12},{12,16},{16,20},{20,24},{24,28},{1,5},{5,9},{9,... | collective-permute-start | bytes 24584 | tf_op jit(solution)/shard_map/ppermute | solution.py:15
  38.5 9.2 %copy-start.1 = (bf16[512,512]{1,0:T(8,128)(2,1)S(1)}, bf16[512,512]{1,0:T(8,128)(2,1)}, u32[]{:S(2)}) copy-start(bf16[512,512]{1,0:T(8,128)(2,1)} %param.18) | copy-start | bytes 1572868
  38.5 9.2 %copy-start.5 = (f32[512]{0:T(512)S(1)}, f32[512]{0:T(512)}, u32[]{:S(2)}) copy-start(f32[512]{0:T(512)} %param.20) | copy-start | bytes 6148
  38.5 9.2 %copy-start.6 = (f32[512]{0:T(512)S(1)}, f32[512]{0:T(512)}, u32[]{:S(2)}) copy-start(f32[512]{0:T(512)} %param.19) | copy-start | bytes 6148
  84.9 38.2 %copy-start.7 = (bf16[1,8,512]{2,1,0:T(8,128)(2,1)S(1)}, bf16[1,8,512]{2,1,0:T(8,128)(2,1)}, u32[]{:S(2)}) copy-start(bf16[1,8,512]{2,1,0:T(8,128)(2,1)} %param.14) | copy-start | bytes 24580
  99.3 97.3 %all-reduce.6.cloned.1.call-start = ((), (), s32[]{:S(2)}) async-start(), calls=%async_computation.2 | async-start | bytes 6291456 | tf_op jit(solution)/shard_map/psum | solution.py:145
  112.6 10.1 %collective-permute-start.2 = (f32[8,512]{1,0:T(8,128)S(1)}, f32[8,512]{1,0:T(8,128)S(1)}, u32[]{:S(2)}, u32[]{:S(2)}) collective-permute-start(f32[8,512]{1,0:T(8,128)S(1)} %get-tuple-element.159), channel_id=1, source_target_pairs={{0,4},{4,8},{8,12},{12,16},{16,20},{20,24},{24,28},{1,5},{5,9},{9,... | collective-permute-start | bytes 49160 | tf_op jit(solution)/shard_map/ppermute | solution.py:27
  117.4 5.6 %collective-permute-start.3 = (f32[8,512]{1,0:T(8,128)S(1)}, f32[8,512]{1,0:T(8,128)S(1)}, u32[]{:S(2)}, u32[]{:S(2)}) collective-permute-start(f32[8,512]{1,0:T(8,128)S(1)} %get-tuple-element.160), channel_id=1, source_target_pairs={{4,0},{8,4},{12,8},{16,12},{20,16},{24,20},{28,24},{5,1},{9,5},{13... | collective-permute-start | bytes 49160 | tf_op jit(solution)/shard_map/ppermute | solution.py:27
  118.9 13.6 %copy-start.2 = (bf16[512,512]{1,0:T(8,128)(2,1)S(1)}, bf16[512,512]{1,0:T(8,128)(2,1)}, u32[]{:S(2)}) copy-start(bf16[512,512]{1,0:T(8,128)(2,1)} %param.16) | copy-start | bytes 1572868
  122.8 10.6 %copy-start.3 = (bf16[512,512]{1,0:T(8,128)(2,1)S(1)}, bf16[512,512]{1,0:T(8,128)(2,1)}, u32[]{:S(2)}) copy-start(bf16[512,512]{1,0:T(8,128)(2,1)} %param.17) | copy-start | bytes 1572868
  124.4 8.9 %copy-start.4 = (bf16[128,512]{1,0:T(8,128)(2,1)S(1)}, bf16[128,512]{1,0:T(8,128)(2,1)}, u32[]{:S(2)}) copy-start(bf16[128,512]{1,0:T(8,128)(2,1)} %reduce-scatter.2.cloned.1.call-done) | copy-start | bytes 393220
Sparse Core Ops, SparseCore 0:
  99.4 23.2 reduce-scatter.1
  126.9 69.6 all-reduce.5
